TPU v7x, 32 devices: a whole 2x2x4 slice. The times are simulated.
32 devices in a mesh: seq: 8 (over y, x, core), tp: 4 (over z).
Axes of the slice: x: 2, y: 2, z: 4, core: 2. Of those that a mesh axis runs over, the one named last changes fastest.
Arguments:
- tokens: bfloat16 [4096, 3584], P('seq'), may hold values from -6 to 6
- norm_gain: float32 [3584], replicated, may hold values from 0.5 to 1.5
- q_weight: bfloat16 [3584, 3584], P(None, 'tp'), may hold values from -0.09375 to 0.09375
- q_bias: float32 [3584], P('tp'), may hold values from -9 to 9
- k_weight: bfloat16 [3584, 512], P(None, 'tp'), may hold values from -0.09375 to 0.09375
- k_bias: float32 [512], P('tp'), may hold values from -9 to 9
- v_weight: bfloat16 [3584, 512], P(None, 'tp'), may hold values from -0.09375 to 0.09375
- v_bias: float32 [512], P('tp'), may hold values from -5 to 5
- o_weight: bfloat16 [3584, 3584], P('tp'), may hold values from -0.09375 to 0.09375
- doc_ids: int32 [4096], replicated, may hold values from 0 to 7, never falling along the last dimension, each value on 1 to 2560 neighbouring positions
Outputs:
- attn_out: bfloat16 [4096, 3584], P('seq', 'tp')
Inputs may be any that keep to these rules, and one draw needn't show every extreme that they name: `doc_ids`: document numbers never fall along the sequence; each document holds 1 to 2560 tokens and one holds exactly that many.
All inputs are finite; a program needn't handle non-finite values.
Results may differ from a plain program's by a relative error of at most 0.012.
Values may be sent and summed in bfloat16 or wider, within the bound.
A program may use at most 128 MiB of HBM per device.

v0:
```python
import jax
import jax.numpy as jnp
from jax import lax
from jax.sharding import PartitionSpec as P

HD = 128


rope_base = 1000000.0


def shifted(value, axis, steps):
    count = lax.axis_size(axis)
    leading, last = (max(0, -steps), min(count, count - steps))
    return lax.ppermute(value, axis, [(source, source + steps) for source in range(leading, last)])


def rotate(t, posf):
    half = t.shape[-1] // 2
    inv = rope_base ** (-(jnp.arange(half, dtype=jnp.float32) * 2.0) / t.shape[-1])
    angle = posf[:, None] * inv[None, :]
    angle = jnp.concatenate([angle, angle], axis=-1)
    turned = jnp.concatenate([-t[..., half:], t[..., :half]], axis=-1)
    return t * jnp.cos(angle)[:, None, :] + turned * jnp.sin(angle)[:, None, :]


def body(
    tokens, norm_gain, q_weight, q_bias, k_weight, k_bias, v_weight, v_bias, o_weight, doc_ids
):
    rows = tokens.shape[0]
    seq_count = lax.axis_size("seq")
    place = lax.axis_index("seq")
    widened = tokens.astype(jnp.float32)
    normed = (
        widened * lax.rsqrt(jnp.mean(widened * widened, axis=-1, keepdims=True) + 1e-06) * norm_gain
    ).astype(jnp.bfloat16)
    local_heads = q_weight.shape[1] // HD
    local_groups = k_weight.shape[1] // HD
    group = local_heads // local_groups
    first_row = place * rows
    qpos = first_row + jnp.arange(rows)
    posf = qpos.astype(jnp.float32)
    query = jnp.dot(normed, q_weight, preferred_element_type=jnp.float32) + q_bias
    query = (
        rotate(query.reshape(rows, local_heads, HD), posf)
        .astype(jnp.bfloat16)
        .reshape(rows, local_groups, group, HD)
    )
    keys = jnp.dot(normed, k_weight, preferred_element_type=jnp.float32) + k_bias
    keys = rotate(keys.reshape(rows, local_groups, HD), posf).astype(jnp.bfloat16)
    values = (
        (jnp.dot(normed, v_weight, preferred_element_type=jnp.float32) + v_bias)
        .astype(jnp.bfloat16)
        .reshape(rows, local_groups, HD)
    )
    qdoc = lax.dynamic_slice_in_dim(doc_ids, first_row, rows, 0)
    last_row = first_row + rows - 1
    scale = 1.0 / HD**0.5

    def absorb(state, kpiece, vpiece, start):
        count = kpiece.shape[0]
        kpos = start + jnp.arange(count)
        kdoc = lax.dynamic_slice_in_dim(doc_ids, start, count, 0)
        needed = (start >= 0) & (start <= last_row) & (kdoc[count - 1] >= qdoc[0])

        def update(current):
            running, total, summed = current
            scores = (
                jnp.einsum("qkgd,tkd->kgqt", query, kpiece, preferred_element_type=jnp.float32)
                * scale
            )
            visible = (kpos[None, :] <= qpos[:, None]) & (qdoc[:, None] == kdoc[None, :])
            scores = jnp.where(visible, scores, -1e30)
            fresh = jnp.maximum(running, jnp.max(scores, axis=-1))
            expd = jnp.where(visible, jnp.exp(scores - fresh[..., None]), 0.0)
            factor = jnp.exp(running - fresh)
            total = total * factor + jnp.sum(expd, axis=-1)
            summed = summed * factor[..., None] + jnp.einsum(
                "kgqt,tkd->kgqd",
                expd.astype(jnp.bfloat16),
                vpiece,
                preferred_element_type=jnp.float32,
            )
            return (fresh, total, summed)

        def unchanged(current):
            return current

        return lax.cond(needed, update, unchanged, state)

    empty = (
        jnp.full((local_groups, group, rows), -1e30, jnp.float32),
        jnp.zeros((local_groups, group, rows), jnp.float32),
        jnp.zeros((local_groups, group, rows, HD), jnp.float32),
    )
    state = absorb(empty, keys, values, first_row)
    reach = (seq_count * rows // 2 + 2 * rows - 2) // rows

    def travel(step, carry):
        stacked, current = carry
        stacked = shifted(stacked, "seq", 1)
        start = first_row - (step + 1) * rows
        return (stacked, absorb(current, stacked[0], stacked[1], start))

    state = lax.fori_loop(0, reach, travel, (jnp.stack([keys, values]), state))[1]
    running, total, summed = state
    normal = summed / total[..., None]
    context = (
        jnp.transpose(normal, (2, 0, 1, 3)).astype(jnp.bfloat16).reshape(rows, local_heads * HD)
    )
    term = jnp.dot(context, o_weight, preferred_element_type=jnp.float32)
    return lax.psum_scatter(term.astype(jnp.bfloat16), "tp", scatter_dimension=1, tiled=True)


def solution(mesh):
    placed = (
        P("seq", None),
        P(),
        P(None, "tp"),
        P("tp"),
        P(None, "tp"),
        P("tp"),
        P(None, "tp"),
        P("tp"),
        P("tp", None),
        P(),
    )
    return jax.shard_map(
        body, mesh=mesh, in_specs=placed, out_specs=P("seq", "tp"), check_vma=False
    )
```

profile of v0, /device:TPU:5, one launch (start us, length us, event | category | flops | bytes accessed | tf_op | source)
XLA Modules:
  0.0 217.5 jit_solution(3707889399572528287)
XLA Ops:
  6.6 3.0 %fusion.38 = f32[512]{0:T(512)S(1)} fusion(bf16[512,3584]{1,0:T(8,128)(2,1)} %param.16), kind=kLoop, calls=%fused_computation.49 | loop fusion | flops 5504512 | bytes 3672064 | tf_op jit(solution)/shard_map/reduce_sum | solution.py:35
  9.6 4.2 %convolution_add_fusion.2 = f32[512,128]{0,1:T(8,128)S(1)} fusion(bf16[3584,128]{1,0:T(8,128)(2,1)S(1)} %copy-done, f32[128]{0:T(128)} %param.21, bf16[512,3584]{1,0:T(8,128)(2,1)} %param.16, f32[3584]{0:T(1024)} %param.17, f32[512]{0:T(512)S(1)} %add_rsqrt_fusion), kind=kOutput, calls=%fused_computation.59 | convolution fusion | flops 477167616 | bytes 4866560 | tf_op jit(solution)/shard_map/dot_general | solution.py:49
  13.9 5.3 %convolution_add_fusion = f32[512,896]{1,0:T(8,128)} fusion(bf16[3584,896]{1,0:T(8,128)(2,1)S(1)} %copy-done.5, f32[896]{0:T(1024)S(1)} %copy-done.7, bf16[512,3584]{1,0:T(8,128)(2,1)S(1)} %copy-done.2, f32[3584]{0:T(1024)S(1)} %copy-done.6, f32[512]{0:T(512)S(1)} %add_rsqrt_fusion), kind=kOutput, calls=%fused_computation.57 | convolution fusion | flops 3296133120 | bytes 11947520 | tf_op jit(solution)/shard_map/dot_general | solution.py:43
  19.2 1.8 copy.36
  21.0 1.5 fusion.44
  22.5 0.8 dynamic_slice.11
  23.3 0.6 fusion.55
  25.3 1.0 fusion.46
  26.3 3.0 %fusion.42 = bf16[512,1,7,128]{0,3,2,1:T(8,128)(2,1)} fusion(f32[512,1,7,64]{0,3,2,1:T(8,128)} %get-tuple-element.405, f32[512,1,7,64]{0,3,2,1:T(8,128)} %get-tuple-element.404, f32[512,1,7,128]{0,3,2,1:T(8,128)S(1)} %bitcast.121, f32[512,128]{0,1:T(8,128)S(1)} %get-tuple-element.410, f32[512,128]{0,1:T(8,128)S(1)} %get-tuple-element.408), kind=kLoop, calls=%fused_computation.55 | loop fusion | flops 2293760 | bytes 5111808 | tf_op jit(solution)/shard_map/convert_element_type | solution.py:46
  29.3 1.6 copy.42
  31.0 3.7 %fusion.43 = bf16[512,128]{0,1:T(8,128)(2,1)S(1)} fusion(bf16[3584,128]{1,0:T(8,128)(2,1)} %param.22, f32[128]{0:T(128)S(1)} %copy-done.8, bf16[512,3584]{1,0:T(8,128)(2,1)} %param.16, f32[3584]{0:T(1024)S(1)} %copy-done.6, f32[512]{0:T(512)S(1)} %add_rsqrt_fusion), kind=kOutput, calls=%fused_computation.60 | convolution fusion | flops 477233152 | bytes 4735488 | tf_op jit(solution)/shard_map/dot_general | solution.py:52
  34.7 0.6 copy-done.3
  35.6 7.3 %conditional.2 = (f32[1,7,512]{2,1,0:T(8,128)S(1)}, f32[1,7,512]{2,1,0:T(8,128)S(1)}, f32[1,7,512,128]{3,2,1,0:T(8,128)}) conditional(s32[]{:T(128)} %convert_element_type.60, () %tuple.34, (s32[512]{0:T(512)S(1)}, s32[512]{0:T(512)S(1)}, bf16[512,1,7,128]{0,3,2,1:T(8,128)(2,1)S(1)}, bf16[512,128]{0,1:T(8,128)(2,1)S(1)}, ...), branch_computations={%region_1.0_spmd, %region_2.5_spmd} | conditional | flops 964642304 | bytes 26783796 | solution.py:89
  36.1 1.4 fusion.2
  37.5 3.6 %add_bitcast_fusion = f32[1,7,512,128]{3,2,1,0:T(8,128)} fusion(f32[512,512,7]{1,0,2:T(8,128)S(1)} %get-tuple-element.399, f32[7,512]{1,0:T(8,128)S(1)} %get-tuple-element.397, pred[512,512]{0,1:T(8,128)(4,1)S(1)} %compare_and_fusion, f32[7,512]{1,0:T(8,128)S(1)} %get-tuple-element.396, bf16[512,128]{0,1:T(8,128)(2,1)S(1)} %copy-done.4), kind=kOutput, calls=%fused_computation.9 | convolution fusion | flops 479395840 | bytes 9596928 | tf_op jit(solution)/shard_map/cond/branch_1_fun/kgqt,tkd->kgqd/dot_general | solution.py:78
  41.1 1.8 fusion.4
  42.9 70.8 %while.21 = (s32[]{:T(128)}, bf16[2,512,1,128]{3,1,2,0:T(8,128)(2,1)S(1)}, f32[1,7,512]{2,1,0:T(8,128)S(1)}, f32[1,7,512]{2,1,0:T(8,128)S(1)}, f32[1,7,512,128]{...) while((s32[]{:T(128)}, ...), condition=%wide.region_10.11_spmd.clone.clone, body=%wide.region_5.10_spmd.clone.clone.sunk | while | flops 965094912 | bytes 29747640 | solution.py:105
  42.9 3.7 %collective-permute-start = (bf16[2,512,1,128]{3,1,2,0:T(8,128)(2,1)S(1)}, bf16[2,512,1,128]{3,1,2,0:T(8,128)(2,1)S(1)}, u32[]{:S(2)}, u32[]{:S(2)}) collective-permute-start(bf16[2,512,1,128]{3,1,2,0:T(8,128)(2,1)S(1)} %get-tuple-element.509), channel_id=1, source_target_pairs={{0,4},{4,8},{8,12},{12,16},{16,20},{20,24},{24,28},{1,5},{5,9},{9,... | collective-permute-start | bytes 786440 | tf_op jit(solution)/shard_map/while/body/eval_jaxpr/ppermute | solution.py:15
  46.6 0.8 dynamic_slice.15
  49.9 8.2 %conditional.6 = ((f32[1,7,512]{2,1,0:T(8,128)S(1)}, f32[1,7,512]{2,1,0:T(8,128)S(1)}, f32[1,7,512,128]{3,2,1,0:T(8,128)})) conditional(s32[]{:T(128)} %convert_element_type.101, (f32[1,7,512]{2,1,0:T(8,128)S(1)}, f32[1,7,512]{2,1,0:T(8,128)S(1)}, f32[1,7,512,128]{3,2,1,0:T(8,128)}) %tuple.75, (s32[]{:T(128)}, s32[512]{0:T(512)S(1)}, s32[]{:T(128)}, ...), branch_computations={%region_6.6_spmd, %region_7.9_spmd} | conditional | flops 965094912 | bytes 28168232 | solution.py:89
  50.2 1.3 fusion.19
  51.5 4.7 %bitcast_add_fusion.1 = f32[1,7,512,128]{3,2,1,0:T(8,128)} fusion(f32[1,7,512,128]{3,2,1,0:T(8,128)} %get-tuple-element.243, f32[512,512,7]{1,0,2:T(8,128)S(1)} %get-tuple-element.401, f32[7,512]{1,0:T(8,128)S(1)} %bitcast.123, pred[512,512]{0,1:T(8,128)(4,1)S(1)} %compare_and_fusion.1, f32[7,512]{1,0:T(8,128)S(1)} %get-tuple-element.394, ...), kind=kOutput, calls=%fused_computation.30 | convolution fusion | flops 479854592 | bytes 11436032 | tf_op jit(solution)/shard_map/while/body/eval_jaxpr/cond/branch_1_fun/kgqt,tkd->kgqd/dot_general | solution.py:78
  56.3 1.8 fusion.21
  58.1 4.4 %collective-permute-start = (bf16[2,512,1,128]{3,1,2,0:T(8,128)(2,1)S(1)}, bf16[2,512,1,128]{3,1,2,0:T(8,128)(2,1)S(1)}, u32[]{:S(2)}, u32[]{:S(2)}) collective-permute-start(bf16[2,512,1,128]{3,1,2,0:T(8,128)(2,1)S(1)} %get-tuple-element.509), channel_id=1, source_target_pairs={{0,4},{4,8},{8,12},{12,16},{16,20},{20,24},{24,28},{1,5},{5,9},{9,... | collective-permute-start | bytes 786440 | tf_op jit(solution)/shard_map/while/body/eval_jaxpr/ppermute | solution.py:15
  62.5 0.8 dynamic_slice.15
  65.8 8.2 %conditional.6 = ((f32[1,7,512]{2,1,0:T(8,128)S(1)}, f32[1,7,512]{2,1,0:T(8,128)S(1)}, f32[1,7,512,128]{3,2,1,0:T(8,128)})) conditional(s32[]{:T(128)} %convert_element_type.101, (f32[1,7,512]{2,1,0:T(8,128)S(1)}, f32[1,7,512]{2,1,0:T(8,128)S(1)}, f32[1,7,512,128]{3,2,1,0:T(8,128)}) %tuple.75, (s32[]{:T(128)}, s32[512]{0:T(512)S(1)}, s32[]{:T(128)}, ...), branch_computations={%region_6.6_spmd, %region_7.9_spmd} | conditional | flops 965094912 | bytes 28168232 | solution.py:89
  66.1 1.3 fusion.19
  67.5 4.7 %bitcast_add_fusion.1 = f32[1,7,512,128]{3,2,1,0:T(8,128)} fusion(f32[1,7,512,128]{3,2,1,0:T(8,128)} %get-tuple-element.243, f32[512,512,7]{1,0,2:T(8,128)S(1)} %get-tuple-element.401, f32[7,512]{1,0:T(8,128)S(1)} %bitcast.123, pred[512,512]{0,1:T(8,128)(4,1)S(1)} %compare_and_fusion.1, f32[7,512]{1,0:T(8,128)S(1)} %get-tuple-element.394, ...), kind=kOutput, calls=%fused_computation.30 | convolution fusion | flops 479854592 | bytes 11436032 | tf_op jit(solution)/shard_map/while/body/eval_jaxpr/cond/branch_1_fun/kgqt,tkd->kgqd/dot_general | solution.py:78
  72.2 1.8 fusion.21
  74.1 4.4 %collective-permute-start = (bf16[2,512,1,128]{3,1,2,0:T(8,128)(2,1)S(1)}, bf16[2,512,1,128]{3,1,2,0:T(8,128)(2,1)S(1)}, u32[]{:S(2)}, u32[]{:S(2)}) collective-permute-start(bf16[2,512,1,128]{3,1,2,0:T(8,128)(2,1)S(1)} %get-tuple-element.509), channel_id=1, source_target_pairs={{0,4},{4,8},{8,12},{12,16},{16,20},{20,24},{24,28},{1,5},{5,9},{9,... | collective-permute-start | bytes 786440 | tf_op jit(solution)/shard_map/while/body/eval_jaxpr/ppermute | solution.py:15
  78.5 0.8 dynamic_slice.15
  81.8 8.2 %conditional.6 = ((f32[1,7,512]{2,1,0:T(8,128)S(1)}, f32[1,7,512]{2,1,0:T(8,128)S(1)}, f32[1,7,512,128]{3,2,1,0:T(8,128)})) conditional(s32[]{:T(128)} %convert_element_type.101, (f32[1,7,512]{2,1,0:T(8,128)S(1)}, f32[1,7,512]{2,1,0:T(8,128)S(1)}, f32[1,7,512,128]{3,2,1,0:T(8,128)}) %tuple.75, (s32[]{:T(128)}, s32[512]{0:T(512)S(1)}, s32[]{:T(128)}, ...), branch_computations={%region_6.6_spmd, %region_7.9_spmd} | conditional | flops 965094912 | bytes 28168232 | solution.py:89
  82.0 1.3 fusion.19
  83.4 4.7 %bitcast_add_fusion.1 = f32[1,7,512,128]{3,2,1,0:T(8,128)} fusion(f32[1,7,512,128]{3,2,1,0:T(8,128)} %get-tuple-element.243, f32[512,512,7]{1,0,2:T(8,128)S(1)} %get-tuple-element.401, f32[7,512]{1,0:T(8,128)S(1)} %bitcast.123, pred[512,512]{0,1:T(8,128)(4,1)S(1)} %compare_and_fusion.1, f32[7,512]{1,0:T(8,128)S(1)} %get-tuple-element.394, ...), kind=kOutput, calls=%fused_computation.30 | convolution fusion | flops 479854592 | bytes 11436032 | tf_op jit(solution)/shard_map/while/body/eval_jaxpr/cond/branch_1_fun/kgqt,tkd->kgqd/dot_general | solution.py:78
  88.2 1.8 fusion.21
  90.0 4.4 %collective-permute-start = (bf16[2,512,1,128]{3,1,2,0:T(8,128)(2,1)S(1)}, bf16[2,512,1,128]{3,1,2,0:T(8,128)(2,1)S(1)}, u32[]{:S(2)}, u32[]{:S(2)}) collective-permute-start(bf16[2,512,1,128]{3,1,2,0:T(8,128)(2,1)S(1)} %get-tuple-element.509), channel_id=1, source_target_pairs={{0,4},{4,8},{8,12},{12,16},{16,20},{20,24},{24,28},{1,5},{5,9},{9,... | collective-permute-start | bytes 786440 | tf_op jit(solution)/shard_map/while/body/eval_jaxpr/ppermute | solution.py:15
  94.4 0.8 dynamic_slice.15
  97.7 8.2 %conditional.6 = ((f32[1,7,512]{2,1,0:T(8,128)S(1)}, f32[1,7,512]{2,1,0:T(8,128)S(1)}, f32[1,7,512,128]{3,2,1,0:T(8,128)})) conditional(s32[]{:T(128)} %convert_element_type.101, (f32[1,7,512]{2,1,0:T(8,128)S(1)}, f32[1,7,512]{2,1,0:T(8,128)S(1)}, f32[1,7,512,128]{3,2,1,0:T(8,128)}) %tuple.75, (s32[]{:T(128)}, s32[512]{0:T(512)S(1)}, s32[]{:T(128)}, ...), branch_computations={%region_6.6_spmd, %region_7.9_spmd} | conditional | flops 965094912 | bytes 28168232 | solution.py:89
  98.0 1.3 fusion.19
  99.4 4.7 %bitcast_add_fusion.1 = f32[1,7,512,128]{3,2,1,0:T(8,128)} fusion(f32[1,7,512,128]{3,2,1,0:T(8,128)} %get-tuple-element.243, f32[512,512,7]{1,0,2:T(8,128)S(1)} %get-tuple-element.401, f32[7,512]{1,0:T(8,128)S(1)} %bitcast.123, pred[512,512]{0,1:T(8,128)(4,1)S(1)} %compare_and_fusion.1, f32[7,512]{1,0:T(8,128)S(1)} %get-tuple-element.394, ...), kind=kOutput, calls=%fused_computation.30 | convolution fusion | flops 479854592 | bytes 11436032 | tf_op jit(solution)/shard_map/while/body/eval_jaxpr/cond/branch_1_fun/kgqt,tkd->kgqd/dot_general | solution.py:78
  104.1 1.8 fusion.21
  105.9 4.4 %collective-permute-start = (bf16[2,512,1,128]{3,1,2,0:T(8,128)(2,1)S(1)}, bf16[2,512,1,128]{3,1,2,0:T(8,128)(2,1)S(1)}, u32[]{:S(2)}, u32[]{:S(2)}) collective-permute-start(bf16[2,512,1,128]{3,1,2,0:T(8,128)(2,1)S(1)} %get-tuple-element.509), channel_id=1, source_target_pairs={{0,4},{4,8},{8,12},{12,16},{16,20},{20,24},{24,28},{1,5},{5,9},{9,... | collective-permute-start | bytes 786440 | tf_op jit(solution)/shard_map/while/body/eval_jaxpr/ppermute | solution.py:15
  110.4 0.8 dynamic_slice.15
  113.7 1.8 copy.43
  115.8 8.3 %convolution_convert_fusion = bf16[512,3584]{1,0:T(8,128)(2,1)} fusion(bf16[512,896]{0,1:T(8,128)(2,1)S(1)} %bitcast.128, bf16[896,3584]{1,0:T(8,128)(2,1)} %param.24), kind=kOutput, calls=%fused_computation.52 | convolution fusion | flops 3290169344 | bytes 11010048 | tf_op jit(solution)/shard_map/dot_general | solution.py:111
  124.1 5.9 %copy.51 = bf16[512,3584]{0,1:T(8,128)(2,1)} copy(bf16[512,3584]{1,0:T(8,128)(2,1)} %convolution_convert_fusion) | data formatting | bytes 7340032
  130.0 78.4 %reduce-scatter.4.cloned.1.call-done = bf16[896,512]{1,0:T(8,128)(2,1)} async-done(((bf16[3584,512]{1,0:T(8,128)(2,1)}), bf16[896,512]{1,0:T(8,128)(2,1)}) %reduce-scatter.4.cloned.1.call-update) | async-done | bytes 917520
  208.5 2.2 %copy.52 = bf16[512,896]{1,0:T(8,128)(2,1)} copy(bf16[512,896]{0,1:T(8,128)(2,1)} %bitcast.127) | data formatting | bytes 1835008
  (76 shorter events, 8.7 us)
Async XLA Ops:
  6.5 3.1 %copy-start = (bf16[3584,128]{1,0:T(8,128)(2,1)S(1)}, bf16[3584,128]{1,0:T(8,128)(2,1)}, u32[]{:S(2)}) copy-start(bf16[3584,128]{1,0:T(8,128)(2,1)} %param.20) | copy-start | bytes 2752516
  6.5 7.3 %copy-start.6 = (f32[3584]{0:T(1024)S(1)}, f32[3584]{0:T(1024)}, u32[]{:S(2)}) copy-start(f32[3584]{0:T(1024)} %param.17) | copy-start | bytes 43012
  6.5 7.4 %copy-start.7 = (f32[896]{0:T(1024)S(1)}, f32[896]{0:T(1024)}, u32[]{:S(2)}) copy-start(f32[896]{0:T(1024)} %param.19) | copy-start | bytes 10756
  6.5 201.9 %reduce-scatter.4.cloned.1.call-start = ((), (), s32[]{:S(2)}) async-start(), calls=%async_computation.1 | async-start | bytes 4587520
  6.6 7.3 %copy-start.2 = (bf16[512,3584]{1,0:T(8,128)(2,1)S(1)}, bf16[512,3584]{1,0:T(8,128)(2,1)}, u32[]{:S(2)}) copy-start(bf16[512,3584]{1,0:T(8,128)(2,1)} %param.16) | copy-start | bytes 11010052
  6.6 7.3 %copy-start.5 = (bf16[3584,896]{1,0:T(8,128)(2,1)S(1)}, bf16[3584,896]{1,0:T(8,128)(2,1)}, u32[]{:S(2)}) copy-start(bf16[3584,896]{1,0:T(8,128)(2,1)} %param.18) | copy-start | bytes 19267588
  19.2 11.8 %copy-start.8 = (f32[128]{0:T(128)S(1)}, f32[128]{0:T(128)}, u32[]{:S(2)}) copy-start(f32[128]{0:T(128)} %param.23) | copy-start | bytes 1540
  29.3 6.1 %copy-start.1 = (bf16[512,1,7,128]{0,3,2,1:T(8,128)(2,1)S(1)}, bf16[512,1,7,128]{0,3,2,1:T(8,128)(2,1)}, u32[]{:S(2)}) copy-start(bf16[512,1,7,128]{0,3,2,1:T(8,128)(2,1)} %fusion.42) | copy-start | bytes 2752516
  34.7 0.7 copy-start.3
  35.8 1.7 copy-start.4
  42.9 7.0 %collective-permute-start = (bf16[2,512,1,128]{3,1,2,0:T(8,128)(2,1)S(1)}, bf16[2,512,1,128]{3,1,2,0:T(8,128)(2,1)S(1)}, u32[]{:S(2)}, u32[]{:S(2)}) collective-permute-start(bf16[2,512,1,128]{3,1,2,0:T(8,128)(2,1)S(1)} %get-tuple-element.509), channel_id=1, source_target_pairs={{0,4},{4,8},{8,12},{12,16},{16,20},{20,24},{24,28},{1,5},{5,9},{9,... | collective-permute-start | bytes 786440 | tf_op jit(solution)/shard_map/while/body/eval_jaxpr/ppermute | solution.py:15
  58.1 7.7 %collective-permute-start = (bf16[2,512,1,128]{3,1,2,0:T(8,128)(2,1)S(1)}, bf16[2,512,1,128]{3,1,2,0:T(8,128)(2,1)S(1)}, u32[]{:S(2)}, u32[]{:S(2)}) collective-permute-start(bf16[2,512,1,128]{3,1,2,0:T(8,128)(2,1)S(1)} %get-tuple-element.509), channel_id=1, source_target_pairs={{0,4},{4,8},{8,12},{12,16},{16,20},{20,24},{24,28},{1,5},{5,9},{9,... | collective-permute-start | bytes 786440 | tf_op jit(solution)/shard_map/while/body/eval_jaxpr/ppermute | solution.py:15
  74.1 7.7 %collective-permute-start = (bf16[2,512,1,128]{3,1,2,0:T(8,128)(2,1)S(1)}, bf16[2,512,1,128]{3,1,2,0:T(8,128)(2,1)S(1)}, u32[]{:S(2)}, u32[]{:S(2)}) collective-permute-start(bf16[2,512,1,128]{3,1,2,0:T(8,128)(2,1)S(1)} %get-tuple-element.509), channel_id=1, source_target_pairs={{0,4},{4,8},{8,12},{12,16},{16,20},{20,24},{24,28},{1,5},{5,9},{9,... | collective-permute-start | bytes 786440 | tf_op jit(solution)/shard_map/while/body/eval_jaxpr/ppermute | solution.py:15
  90.0 7.7 %collective-permute-start = (bf16[2,512,1,128]{3,1,2,0:T(8,128)(2,1)S(1)}, bf16[2,512,1,128]{3,1,2,0:T(8,128)(2,1)S(1)}, u32[]{:S(2)}, u32[]{:S(2)}) collective-permute-start(bf16[2,512,1,128]{3,1,2,0:T(8,128)(2,1)S(1)} %get-tuple-element.509), channel_id=1, source_target_pairs={{0,4},{4,8},{8,12},{12,16},{16,20},{20,24},{24,28},{1,5},{5,9},{9,... | collective-permute-start | bytes 786440 | tf_op jit(solution)/shard_map/while/body/eval_jaxpr/ppermute | solution.py:15
  105.9 7.7 %collective-permute-start = (bf16[2,512,1,128]{3,1,2,0:T(8,128)(2,1)S(1)}, bf16[2,512,1,128]{3,1,2,0:T(8,128)(2,1)S(1)}, u32[]{:S(2)}, u32[]{:S(2)}) collective-permute-start(bf16[2,512,1,128]{3,1,2,0:T(8,128)(2,1)S(1)} %get-tuple-element.509), channel_id=1, source_target_pairs={{0,4},{4,8},{8,12},{12,16},{16,20},{20,24},{24,28},{1,5},{5,9},{9,... | collective-permute-start | bytes 786440 | tf_op jit(solution)/shard_map/while/body/eval_jaxpr/ppermute | solution.py:15
Sparse Core Ops, SparseCore 0:
  130.2 78.2 reduce-scatter.3
where the time goes:
time: 220 us; the launch traced here: 218 us
  waiting for transfers between devices  79.2 us (36%)
  matrix products  50.8 us (23%)
  local copies, waits for them, and re-layouts  25.3 us (12%)
  starting transfers between devices  21.2 us (10%)
  other arithmetic  19.2 us (9%)
  between operations  14.9 us (7%)
  loops' own time  6.88 us (3%)
    unnamed x2, waiting for transfers between devices  78.5 us
    dot_general x5, matrix products, update(): jnp.einsum('kgqt,tkd->kgqd', expd.astype(jnp.bfloat16), vpiece, preferred...  22.5 us
    ppermute x5, starting transfers between devices, shifted(): lax.ppermute(value, axis, [(source, source + steps) for source in range(l...  21.2 us
    unnamed x20, local copies, waits for them, and re-layouts  10.6 us
    reduce_sum x5, other arithmetic, update(): total = total * factor + jnp.sum(expd, axis=-1)  8.78 us
    dot_general x1, matrix products, body(): term = jnp.dot(context, o_weight, preferred_element_type=jnp.float32)  8.3 us
    dot_general x5, matrix products, update(): jnp.einsum('qkgd,tkd->kgqt', query, kpiece, preferred_element_type=jnp.fl...  6.79 us
    another operation x1, loops' own time, body(): lax.fori_loop(0, reach, travel, (jnp.stack([keys, values]), state))[1]  6.47 us
  transfers between devices with their start and end apart: 6, of which 6 were waited for; matrix products, arithmetic and copies ran while one was open for 4% of the time, Pallas kernels for 0%

commit v1 on v0

v1 whole, which is shorter than its diff:
```python
import functools
import math

import jax
import jax.numpy as jnp
from jax import lax
from jax.experimental import pallas as pl
from jax.experimental.pallas import tpu as pltpu
from jax.sharding import PartitionSpec as P

HD = 128
MESH = pl.DeviceIdType.MESH
rope_base = 1000000.0
VMEM = pltpu.VMEM
LAG = 1


def rope_tables(first_row, rows):
    half = HD // 2
    inv = rope_base ** (-(jnp.arange(half, dtype=jnp.float32) * 2.0) / HD)
    posf = (first_row + jnp.arange(rows)).astype(jnp.float32)
    angle = posf[:, None] * inv[None, :]
    cos, sin = jnp.cos(angle), jnp.sin(angle)
    return jnp.concatenate([cos, cos], axis=-1), jnp.concatenate([-sin, sin], axis=-1)


def project(
    tokens_hbm, gain_ref, wq_hbm, qb_ref, wk_hbm, kb_ref, wv_hbm, vb_ref, cos_ref, sin_ref,
    q_ref, kv_ref, tokens, normed, wq, wkv, sems,
):
    width = wq.shape[1]
    step = 2 * HD
    spans = [(lo, min(step, width - lo)) for lo in range(0, width, step)]
    copies = [
        pltpu.make_async_copy(tokens_hbm, tokens, sems.at[0]),
        pltpu.make_async_copy(wk_hbm, wkv.at[:, pl.ds(0, HD)], sems.at[1]),
        pltpu.make_async_copy(wv_hbm, wkv.at[:, pl.ds(HD, HD)], sems.at[2]),
    ]
    for index, (lo, size) in enumerate(spans):
        cut = pl.ds(lo, size)
        copies.append(pltpu.make_async_copy(wq_hbm.at[:, cut], wq.at[:, cut], sems.at[3 + index]))
    for copy in copies:
        copy.start()
    copies[0].wait()
    rows = tokens.shape[0]
    piece = 64

    @pl.loop(0, rows // piece)
    def _(index):
        cut = pl.ds(pl.multiple_of(index * piece, piece), piece)
        wide = tokens[cut, :].astype(jnp.float32)
        mean = jnp.mean(wide * wide, axis=-1, keepdims=True)
        normed[cut, :] = (wide * lax.rsqrt(mean + 1e-06) * gain_ref[...]).astype(jnp.bfloat16)

    cos, sin = cos_ref[...], sin_ref[...]

    def rope(t):
        return (t * cos + pltpu.roll(t, HD // 2, 1) * sin).astype(jnp.bfloat16)

    copies[1].wait()
    copies[2].wait()
    kv = jnp.dot(normed[...], wkv[...], preferred_element_type=jnp.float32)
    kv_ref[0] = rope(kv[:, :HD] + kb_ref[...])
    kv_ref[1] = (kv[:, HD:] + vb_ref[...]).astype(jnp.bfloat16)
    for index, (lo, size) in enumerate(spans):
        copies[3 + index].wait()
        out = jnp.dot(
            normed[...], wq[:, lo:lo + size], preferred_element_type=jnp.float32
        ) + qb_ref[:, lo:lo + size]
        for head in range(0, size, HD):
            q_ref[:, lo + head:lo + head + HD] = rope(out[:, head:head + HD])


def attend(
    seq_count, tp_count, reach, chunk,
    q_ref, kv_ref, kdoc_ref, qdoc_ref, wo_hbm, out_ref,
    wo, kv_in, sent, got, own, wo_sem, kv_send, kv_recv, send_sem, recv_sem,
):
    place = lax.axis_index("seq")
    turn = lax.axis_index("tp")
    rows, width = q_ref.shape
    heads = width // HD
    cols = out_ref.shape[1]
    parts = rows // chunk
    load = pltpu.make_async_copy(wo_hbm, wo, wo_sem)
    load.start()

    barrier = pltpu.get_barrier_semaphore()
    for away in range(1, reach + 1):
        @pl.when(place >= away)
        def _():
            pl.semaphore_signal(barrier, inc=1, device_id={"seq": place - away}, device_id_type=MESH)

        @pl.when(place + away < seq_count)
        def _():
            pl.semaphore_signal(barrier, inc=1, device_id={"seq": place + away}, device_id_type=MESH)

    @pl.when(turn > 0)
    def _():
        pl.semaphore_signal(barrier, inc=1, device_id={"tp": turn - 1}, device_id_type=MESH)

    @pl.when(turn < tp_count - 1)
    def _():
        pl.semaphore_signal(barrier, inc=1, device_id={"tp": turn + 1}, device_id_type=MESH)

    behind = jnp.minimum(place, reach)
    ahead = jnp.minimum(seq_count - 1 - place, reach)
    sides = jnp.where(turn > 0, 1, 0) + jnp.where(turn < tp_count - 1, 1, 0)
    pl.semaphore_wait(barrier, behind + ahead + sides)

    def kv_copy(away):
        return pltpu.make_async_remote_copy(
            src_ref=kv_ref, dst_ref=kv_in.at[away - 1],
            send_sem=kv_send.at[away - 1], recv_sem=kv_recv.at[away - 1],
            device_id={"seq": lax.rem(place + away, seq_count)}, device_id_type=MESH,
        )

    for away in range(1, reach + 1):
        @pl.when(place + away < seq_count)
        def _():
            kv_copy(away).start()

    def term_copy(side, dest, part):
        cut = pl.ds(pl.multiple_of(part * chunk, chunk), chunk)
        target = lax.rem(turn + (1 if side == 0 else tp_count - 1), tp_count)
        return pltpu.make_async_remote_copy(
            src_ref=sent.at[dest, cut], dst_ref=got.at[side, dest, cut],
            send_sem=send_sem.at[dest, part], recv_sem=recv_sem.at[side, dest, part],
            device_id={"tp": target}, device_id_type=MESH,
        )

    factor = math.log2(math.e) / HD**0.5
    order = sorted(range(tp_count), key=lambda d: (-abs(2 * d - tp_count + 1), -d))

    def forward(part):
        cut = pl.ds(pl.multiple_of(part * chunk, chunk), chunk)
        for dest in order:
            for side in (0, 1):
                inner = (turn > 0) & (dest > turn) if side == 0 else (
                    (turn < tp_count - 1) & (dest < turn))

                @pl.when(inner)
                def _():
                    term_copy(side, dest, part).wait_recv()
                    sent[dest, cut] = (
                        sent[dest, cut].astype(jnp.float32) + got[side, dest, cut].astype(jnp.float32)
                    ).astype(jnp.bfloat16)
                    term_copy(side, dest, part).start()

    def finish(part):
        cut = pl.ds(pl.multiple_of(part * chunk, chunk), chunk)
        for dest in range(tp_count):
            for side in (0, 1):
                edge = (turn > 0) if side == 0 else (turn < tp_count - 1)

                @pl.when((dest == turn) & edge)
                def _():
                    term_copy(side, dest, part).wait_recv()
                    own[cut, :] = own[cut, :] + got[side, dest, cut].astype(jnp.float32)

        out_ref[cut, :] = own[cut, :].astype(jnp.bfloat16)

    def piece(part):
        cut = pl.ds(pl.multiple_of(part * chunk, chunk), chunk)
        q = jnp.concatenate([q_ref[cut, h * HD:(h + 1) * HD] for h in range(heads)], axis=0)
        qdoc = qdoc_ref[cut, :]

        def block(state, k, v, visible):
            top, total, summed = state
            s = lax.dot_general(q, k, (((1,), (1,)), ((), ())), preferred_element_type=jnp.float32)
            s = s.reshape(heads, chunk, rows) * factor
            s = jnp.where(visible[None], s, -1e30)
            fresh = jnp.maximum(top, jnp.max(s, axis=-1, keepdims=True))
            e = jnp.exp2(s - fresh)
            scale = jnp.exp2(top - fresh)
            total = total * scale + jnp.sum(e, axis=-1, keepdims=True)
            pv = jnp.dot(
                e.astype(jnp.bfloat16).reshape(heads * chunk, rows), v,
                preferred_element_type=jnp.float32,
            )
            return fresh, total, summed * scale + pv.reshape(heads, chunk, HD)

        row = part * chunk + lax.broadcasted_iota(jnp.int32, (chunk, rows), 0)
        col = lax.broadcasted_iota(jnp.int32, (chunk, rows), 1)
        state = (
            jnp.full((heads, chunk, 1), -1e30, jnp.float32),
            jnp.zeros((heads, chunk, 1), jnp.float32),
            jnp.zeros((heads, chunk, HD), jnp.float32),
        )
        state = block(
            state, kv_ref[0], kv_ref[1], (col <= row) & (qdoc == kdoc_ref[place])
        )

        def earlier(away, state):
            @pl.when(part == 0)
            def _():
                kv_copy(away).wait_recv()

            return block(
                state, kv_in[away - 1, 0], kv_in[away - 1, 1], qdoc == kdoc_ref[place - away]
            )

        _, total, summed = lax.fori_loop(1, behind + 1, earlier, state)
        context = (summed / total).astype(jnp.bfloat16)
        context = jnp.concatenate([context[h] for h in range(heads)], axis=1)

        @pl.when(part == 0)
        def _():
            load.wait()

        for dest in order:
            term = jnp.dot(
                context, wo[:, dest * cols:(dest + 1) * cols], preferred_element_type=jnp.float32
            )

            @pl.when(dest == turn)
            def _():
                own[cut, :] = term

            @pl.when(dest != turn)
            def _():
                sent[dest, cut] = term.astype(jnp.bfloat16)

            @pl.when((turn == 0) & (dest > 0))
            def _():
                term_copy(0, dest, part).start()

            @pl.when((turn == tp_count - 1) & (dest < tp_count - 1))
            def _():
                term_copy(1, dest, part).start()

    @pl.loop(0, parts + LAG)
    def _(part):
        @pl.when(part < parts)
        def _():
            piece(part)

        @pl.when(part >= LAG)
        def _():
            forward(part - LAG)

    @pl.loop(0, parts)
    def _(part):
        finish(part)

    @pl.loop(0, parts)
    def _(part):
        for dest in range(tp_count):
            @pl.when(dest != turn)
            def _():
                term_copy(0, dest, part).wait_send()

    for away in range(1, reach + 1):
        @pl.when(place + away < seq_count)
        def _():
            kv_copy(away).wait_send()


def body(
    tokens, norm_gain, q_weight, q_bias, k_weight, k_bias, v_weight, v_bias, o_weight, doc_ids
):
    rows, model = tokens.shape
    seq_count = lax.axis_size("seq")
    tp_count = lax.axis_size("tp")
    place = lax.axis_index("seq")
    width = q_weight.shape[1]
    cols = o_weight.shape[1] // tp_count
    reach = min(seq_count - 1, (seq_count * rows // 2 + 2 * rows - 2) // rows)
    chunk = rows // 4
    parts = rows // chunk
    cos, sin = rope_tables(place * rows, rows)
    hbm = pl.BlockSpec(memory_space=pl.ANY)
    vmem = pl.BlockSpec(memory_space=VMEM)
    limit = 56 * 1024 * 1024
    query, kv = pl.pallas_call(
        project,
        out_shape=(
            jax.ShapeDtypeStruct((rows, width), jnp.bfloat16),
            jax.ShapeDtypeStruct((2, rows, HD), jnp.bfloat16),
        ),
        in_specs=[hbm, vmem, hbm, vmem, hbm, vmem, hbm, vmem, vmem, vmem],
        out_specs=(vmem, vmem),
        scratch_shapes=[
            VMEM((rows, model), jnp.bfloat16),
            VMEM((rows, model), jnp.bfloat16),
            VMEM((model, width), jnp.bfloat16),
            VMEM((model, 2 * HD), jnp.bfloat16),
            pltpu.SemaphoreType.DMA((3 + -(-width // (2 * HD)),)),
        ],
        compiler_params=pltpu.CompilerParams(vmem_limit_bytes=limit),
    )(
        tokens, norm_gain[None], q_weight, q_bias[None], k_weight, k_bias[None],
        v_weight, v_bias[None], cos, sin,
    )
    qdoc = lax.dynamic_slice_in_dim(doc_ids, place * rows, rows, 0)[:, None]
    kdoc = doc_ids.reshape(seq_count, 1, rows)
    return pl.pallas_call(
        functools.partial(attend, seq_count, tp_count, reach, chunk),
        out_shape=jax.ShapeDtypeStruct((rows, cols), jnp.bfloat16),
        in_specs=[vmem, vmem, vmem, vmem, hbm],
        out_specs=vmem,
        scratch_shapes=[
            VMEM(o_weight.shape, jnp.bfloat16),
            VMEM((reach, 2, rows, HD), jnp.bfloat16),
            VMEM((tp_count, rows, cols), jnp.bfloat16),
            VMEM((2, tp_count, rows, cols), jnp.bfloat16),
            VMEM((rows, cols), jnp.float32),
            pltpu.SemaphoreType.DMA,
            pltpu.SemaphoreType.DMA((reach,)),
            pltpu.SemaphoreType.DMA((reach,)),
            pltpu.SemaphoreType.DMA((tp_count, parts)),
            pltpu.SemaphoreType.DMA((2, tp_count, parts)),
        ],
        compiler_params=pltpu.CompilerParams(
            collective_id=0, has_side_effects=True, vmem_limit_bytes=limit
        ),
    )(query, kv, kdoc, qdoc, o_weight)


def solution(mesh):
    placed = (
        P("seq", None),
        P(),
        P(None, "tp"),
        P("tp"),
        P(None, "tp"),
        P("tp"),
        P(None, "tp"),
        P("tp"),
        P("tp", None),
        P(),
    )
    return jax.shard_map(
        body, mesh=mesh, in_specs=placed, out_specs=P("seq", "tp"), check_vma=False
    )
```

time: 220 us -> 128 us (0.58)
  Pallas kernels: 0 us -> 119 us
  waiting for transfers between devices: 79.2 us -> 0 us
  matrix products: 50.8 us -> 0 us
  starting transfers between devices: 21.2 us -> 0 us
  local copies, waits for them, and re-layouts: 25.3 us -> 6.4 us
  other arithmetic: 19.2 us -> 2 us
  between operations: 14.9 us -> 0.03 us
  loops' own time: 6.88 us -> 0 us
    pallas_call x0 -> x2, Pallas kernels: none -> 119 us  [the longest x1 104 us: body(): pl.pallas_call(functools.partial(attend, seq_count, tp_count, reach, chun...]
    unnamed x2 -> x0, waiting for transfers between devices: 78.5 us -> none
    dot_general x14 -> x0, matrix products: 50.8 us -> none  [the longest x5 22.5 us: update(): jnp.einsum('kgqt,tkd->kgqd', expd.astype(jnp.bfloat16), vpiece, preferred...]
    ppermute x5 -> x0, starting transfers between devices: 21.2 us -> none  [shifted(): lax.ppermute(value, axis, [(source, source + steps) for source in range(l...]
    reduce_sum x6 -> x0, other arithmetic: 11.8 us -> none  [the longest x5 8.78 us: update(): total = total * factor + jnp.sum(expd, axis=-1)]
    unnamed x20 -> x1, local copies, waits for them, and re-layouts: 10.6 us -> 2.18 us
    another operation x7 -> x0, loops' own time: 6.88 us -> none  [the longest x1 6.47 us: body(): lax.fori_loop(0, reach, travel, (jnp.stack([keys, values]), state))[1]]
    slice x11 -> x0, local copies, waits for them, and re-layouts: 6.31 us -> none  [absorb(): needed = (start >= 0) & (start <= last_row) & (kdoc[count - 1] >= qdoc[0])]
  transfers between devices with their start and end apart: 6 -> 0, of which waited for: 6 -> 0; matrix products, arithmetic and copies ran while one was open for 4% -> 0% of each run, Pallas kernels for 0% -> 0%
where the time goes in v1:
time: 128 us
  Pallas kernels  119 us (93%)
  local copies, waits for them, and re-layouts  6.4 us (5%)
  other arithmetic  2 us (2%)
    pallas_call x1, Pallas kernels, body(): pl.pallas_call(functools.partial(attend, seq_count, tp_count, reach, chun...  104 us
    pallas_call x1, Pallas kernels, body(): pl.pallas_call(project, out_shape=(jax.ShapeDtypeStruct((rows, width), jn...  15.4 us

profile of v1, /device:TPU:5, one launch (start us, length us, event | category | flops | bytes accessed | tf_op | source)
XLA Modules:
  0.0 127.7 jit_solution(10638405172154236385)
XLA Ops:
  0.0 0.8 dynamic_slice.3
  0.8 1.3 %broadcast_in_dim.18.qb_ref = f32[1,896]{1,0:T(1,128)} reshape(f32[896]{0:T(1024)} %param.13) | data formatting | bytes 7168 | tf_op jit(solution)/shard_map/broadcast_in_dim | solution.py:292
  2.1 1.3 %broadcast_in_dim.17.gain_ref = f32[1,3584]{1,0:T(1,128)} reshape(f32[3584]{0:T(1024)} %param.11) | data formatting | bytes 28672 | tf_op jit(solution)/shard_map/broadcast_in_dim | solution.py:292
  3.4 0.9 copy.11.qdoc_ref
  4.2 1.0 fusion
  5.2 1.0 pad_maximum_fusion
  6.2 15.4 %shard_map.100 = (bf16[512,896]{1,0:T(8,128)(2,1)}, bf16[2,512,128]{2,1,0:T(8,128)(2,1)}) custom-call(bf16[512,3584]{1,0:T(8,128)(2,1)} %tokens_hbm.1, f32[1,3584]{1,0:T(1,128)} %broadcast_in_dim.17.gain_ref, bf16[3584,896]{1,0:T(8,128)(2,1)} %wq_hbm.1, f32[1,896]{1,0:T(1,128)} %broadcast_in_dim.18.qb_ref, bf16[3584,128]{1,0:T(8,128)(2,1)} %wk_hbm.1, ...), custom_call_target="tpu_custom_call" | custom-call | tf_op jit(solution)/shard_map/pallas_call | solution.py:275
  21.7 103.9 %shard_map.101 = bf16[512,896]{1,0:T(8,128)(2,1)} custom-call(bf16[512,896]{1,0:T(8,128)(2,1)} %get-tuple-element.7.q_ref, bf16[2,512,128]{2,1,0:T(8,128)(2,1)} %get-tuple-element.8.kv_ref, s32[8,1,512]{2,1,0:T(1,128)} %bitcast.4, s32[512,1]{1,0:T(8,128)} %copy.11.qdoc_ref, bf16[896,3584]{1,0:T(8,128)(2,1)} %wo_hbm.1), custom_call_target="tpu_custom_call" | custom-call | tf_op jit(solution)/shard_map/pallas_call | solution.py:297
  125.5 2.2 %copy.13 = bf16[512,896]{1,0:T(8,128)(2,1)} copy(bf16[512,896]{1,0:T(8,128)(2,1)} %shard_map.101) | data formatting | bytes 1835008
  (2 shorter events, 0.0 us)

commit v2 on v1

v2 whole, which is shorter than its diff:
```python
import functools
import math

import jax
import jax.numpy as jnp
import numpy as np
from jax import lax
from jax.experimental import pallas as pl
from jax.experimental.pallas import tpu as pltpu
from jax.sharding import PartitionSpec as P

HD = 128
MESH = pl.DeviceIdType.MESH
rope_base = 1000000.0
VMEM = pltpu.VMEM
LAG = 1


def rope_tables(rows, blocks):
    half = HD // 2
    inv = rope_base ** (-(np.arange(half, dtype=np.float64) * 2.0) / HD)
    inv = np.concatenate([inv, inv])[None, :]
    near = np.arange(rows)[:, None] * inv
    far = np.arange(blocks)[:, None] * rows * inv
    near = np.stack([np.cos(near), np.sin(near)]).astype(np.float32)
    far = np.stack([np.cos(far), np.sin(far)])[:, :, None, :].astype(np.float32)
    return near, far


def attend(
    seq_count, tp_count, reach, chunk,
    tokens_hbm, gain_ref, wq_hbm, qb_ref, wk_hbm, kb_ref, wv_hbm, vb_ref, wo_hbm,
    kdoc_ref, near_hbm, far_ref, out_ref,
    tokens, normed, wq, wkv, wo, near, q_ref, kv_ref, kv_in, sent, got, own,
    load_sems, kv_send, kv_pass, kv_recv, send_sem, recv_sem,
):
    place = lax.axis_index("seq")
    turn = lax.axis_index("tp")
    rows, width = q_ref.shape
    heads = width // HD
    cols = out_ref.shape[1]
    parts = rows // chunk
    step = 2 * HD
    spans = [(lo, min(step, width - lo)) for lo in range(0, width, step)]
    loads = [
        pltpu.make_async_copy(tokens_hbm, tokens, load_sems.at[0]),
        pltpu.make_async_copy(wk_hbm, wkv.at[:, pl.ds(0, HD)], load_sems.at[1]),
        pltpu.make_async_copy(wv_hbm, wkv.at[:, pl.ds(HD, HD)], load_sems.at[2]),
        pltpu.make_async_copy(near_hbm, near, load_sems.at[3]),
    ]
    for index, (lo, size) in enumerate(spans):
        cut = pl.ds(lo, size)
        loads.append(
            pltpu.make_async_copy(wq_hbm.at[:, cut], wq.at[:, cut], load_sems.at[4 + index])
        )
    load = pltpu.make_async_copy(wo_hbm, wo, load_sems.at[4 + len(spans)])
    loads.append(load)
    for copy in loads:
        copy.start()

    barrier = pltpu.get_barrier_semaphore()
    span = min(reach + 1, seq_count - 1)
    for away in range(1, span + 1):
        @pl.when(place >= away)
        def _():
            pl.semaphore_signal(barrier, inc=1, device_id={"seq": place - away}, device_id_type=MESH)

        @pl.when(place + away < seq_count)
        def _():
            pl.semaphore_signal(barrier, inc=1, device_id={"seq": place + away}, device_id_type=MESH)

    @pl.when(turn > 0)
    def _():
        pl.semaphore_signal(barrier, inc=1, device_id={"tp": turn - 1}, device_id_type=MESH)

    @pl.when(turn < tp_count - 1)
    def _():
        pl.semaphore_signal(barrier, inc=1, device_id={"tp": turn + 1}, device_id_type=MESH)

    behind = jnp.minimum(place, reach)
    near_count = jnp.minimum(place, span) + jnp.minimum(seq_count - 1 - place, span)
    sides = jnp.where(turn > 0, 1, 0) + jnp.where(turn < tp_count - 1, 1, 0)

    loads[0].wait()
    slab = 64
    gain = gain_ref[...].reshape(1, gain_ref.shape[0])

    @pl.loop(0, rows // slab)
    def _(index):
        cut = pl.ds(pl.multiple_of(index * slab, slab), slab)
        wide = tokens[cut, :].astype(jnp.float32)
        mean = jnp.mean(wide * wide, axis=-1, keepdims=True)
        normed[cut, :] = (wide * lax.rsqrt(mean + 1e-06) * gain).astype(jnp.bfloat16)

    loads[3].wait()
    far_cos, far_sin = far_ref[0, place], far_ref[1, place]
    cos = near[0] * far_cos - near[1] * far_sin
    sin = near[1] * far_cos + near[0] * far_sin
    lane = lax.broadcasted_iota(jnp.int32, (rows, HD), 1)
    near[0] = cos
    near[1] = jnp.where(lane < HD // 2, -sin, sin)

    def rope(t):
        return (t * near[0] + pltpu.roll(t, HD // 2, 1) * near[1]).astype(jnp.bfloat16)

    loads[1].wait()
    loads[2].wait()
    kv = jnp.dot(normed[...], wkv[...], preferred_element_type=jnp.float32)
    kv_ref[0] = rope(kv[:, :HD] + kb_ref[...].reshape(1, HD))
    kv_ref[1] = (kv[:, HD:] + vb_ref[...].reshape(1, HD)).astype(jnp.bfloat16)

    pl.semaphore_wait(barrier, near_count + sides)

    odd = lax.rem(place, 2) == 1
    partner = place + 1 - 2 * lax.rem(place, 2)

    def kv_copy(away):
        return pltpu.make_async_remote_copy(
            src_ref=kv_ref, dst_ref=kv_in.at[away - 1],
            send_sem=kv_send.at[away - 1], recv_sem=kv_recv.at[away - 1],
            device_id={"seq": lax.rem(place + away, seq_count)}, device_id_type=MESH,
        )

    def relay(away, landing):
        return pltpu.make_async_remote_copy(
            src_ref=kv_in.at[away - 1], dst_ref=kv_in.at[landing - 1],
            send_sem=kv_pass.at[away - 1], recv_sem=kv_recv.at[landing - 1],
            device_id={"seq": partner}, device_id_type=MESH,
        )

    evens = [away for away in range(2, reach + 2, 2) if away < seq_count]

    def wanted(away):
        return odd if away > reach else (place >= 0)

    def each_send(act):
        for away in evens:
            @pl.when((place + away < seq_count) & wanted(away))
            def _():
                act(kv_copy(away))

        @pl.when(jnp.logical_not(odd))
        def _():
            act(kv_copy(1))

    def each_relay(act):
        for away in evens:
            if away + 1 <= reach:
                @pl.when((place >= away) & jnp.logical_not(odd))
                def _():
                    act(relay(away, away + 1))

            @pl.when((place >= away) & odd)
            def _():
                act(relay(away, away - 1))

    each_send(lambda copy: copy.start())

    for index, (lo, size) in enumerate(spans):
        loads[4 + index].wait()
        out = jnp.dot(
            normed[...], wq[:, lo:lo + size], preferred_element_type=jnp.float32
        ) + qb_ref[lo:lo + size].reshape(1, size)
        for head in range(0, size, HD):
            q_ref[:, lo + head:lo + head + HD] = rope(out[:, head:head + HD])

    for away in evens:
        @pl.when((place >= away) & wanted(away))
        def _():
            kv_copy(away).wait_recv()

        if away + 1 <= reach:
            @pl.when((place >= away) & jnp.logical_not(odd))
            def _():
                relay(away, away + 1).start()

        @pl.when((place >= away) & odd)
        def _():
            relay(away, away - 1).start()

    def term_copy(side, dest, part):
        cut = pl.ds(pl.multiple_of(part * chunk, chunk), chunk)
        target = lax.rem(turn + (1 if side == 0 else tp_count - 1), tp_count)
        return pltpu.make_async_remote_copy(
            src_ref=sent.at[dest, cut], dst_ref=got.at[side, dest, cut],
            send_sem=send_sem.at[dest, part], recv_sem=recv_sem.at[side, dest, part],
            device_id={"tp": target}, device_id_type=MESH,
        )

    factor = math.log2(math.e) / HD**0.5
    order = sorted(range(tp_count), key=lambda d: (-abs(2 * d - tp_count + 1), -d))

    def forward(part):
        cut = pl.ds(pl.multiple_of(part * chunk, chunk), chunk)
        for dest in order:
            for side in (0, 1):
                inner = (turn > 0) & (dest > turn) if side == 0 else (
                    (turn < tp_count - 1) & (dest < turn))

                @pl.when(inner)
                def _():
                    term_copy(side, dest, part).wait_recv()
                    sent[dest, cut] = (
                        sent[dest, cut].astype(jnp.float32) + got[side, dest, cut].astype(jnp.float32)
                    ).astype(jnp.bfloat16)
                    term_copy(side, dest, part).start()

    def finish(part):
        cut = pl.ds(pl.multiple_of(part * chunk, chunk), chunk)
        for dest in range(tp_count):
            for side in (0, 1):
                edge = (turn > 0) if side == 0 else (turn < tp_count - 1)

                @pl.when((dest == turn) & edge)
                def _():
                    term_copy(side, dest, part).wait_recv()
                    own[cut, :] = own[cut, :] + got[side, dest, cut].astype(jnp.float32)

        out_ref[cut, :] = own[cut, :].astype(jnp.bfloat16)

    def piece(part):
        cut = pl.ds(pl.multiple_of(part * chunk, chunk), chunk)
        q = jnp.concatenate([q_ref[cut, h * HD:(h + 1) * HD] for h in range(heads)], axis=0)
        lanes = kdoc_ref[place, :, cut].astype(jnp.float32)
        qdoc = jnp.broadcast_to(lanes, (chunk, chunk)).T[:, :1]

        def block(state, k, v, visible):
            top, total, summed = state
            s = lax.dot_general(q, k, (((1,), (1,)), ((), ())), preferred_element_type=jnp.float32)
            s = s.reshape(heads, chunk, rows) * factor
            s = jnp.where(visible[None], s, -1e30)
            fresh = jnp.maximum(top, jnp.max(s, axis=-1, keepdims=True))
            e = jnp.exp2(s - fresh)
            scale = jnp.exp2(top - fresh)
            total = total * scale + jnp.sum(e, axis=-1, keepdims=True)
            pv = jnp.dot(
                e.astype(jnp.bfloat16).reshape(heads * chunk, rows), v,
                preferred_element_type=jnp.float32,
            )
            return fresh, total, summed * scale + pv.reshape(heads, chunk, HD)

        row = part * chunk + lax.broadcasted_iota(jnp.int32, (chunk, rows), 0)
        col = lax.broadcasted_iota(jnp.int32, (chunk, rows), 1)
        state = (
            jnp.full((heads, chunk, 1), -1e30, jnp.float32),
            jnp.zeros((heads, chunk, 1), jnp.float32),
            jnp.zeros((heads, chunk, HD), jnp.float32),
        )
        state = block(
            state, kv_ref[0], kv_ref[1], (col <= row) & (qdoc == kdoc_ref[place].astype(jnp.float32))
        )

        def earlier(away, state):
            @pl.when((part == 0) & (lax.rem(away, 2) == 1))
            def _():
                kv_copy(away).wait_recv()

            return block(
                state, kv_in[away - 1, 0], kv_in[away - 1, 1],
                qdoc == kdoc_ref[place - away].astype(jnp.float32),
            )

        _, total, summed = lax.fori_loop(1, behind + 1, earlier, state)
        context = (summed / total).astype(jnp.bfloat16)
        context = jnp.concatenate([context[h] for h in range(heads)], axis=1)

        @pl.when(part == 0)
        def _():
            load.wait()

        for dest in order:
            term = jnp.dot(
                context, wo[:, dest * cols:(dest + 1) * cols], preferred_element_type=jnp.float32
            )

            @pl.when(dest == turn)
            def _():
                own[cut, :] = term

            @pl.when(dest != turn)
            def _():
                sent[dest, cut] = term.astype(jnp.bfloat16)

            @pl.when((turn == 0) & (dest > 0))
            def _():
                term_copy(0, dest, part).start()

            @pl.when((turn == tp_count - 1) & (dest < tp_count - 1))
            def _():
                term_copy(1, dest, part).start()

    @pl.loop(0, parts + LAG)
    def _(part):
        @pl.when(part < parts)
        def _():
            piece(part)

        @pl.when(part >= LAG)
        def _():
            forward(part - LAG)

    @pl.loop(0, parts)
    def _(part):
        finish(part)

    @pl.loop(0, parts)
    def _(part):
        for dest in range(tp_count):
            @pl.when(dest != turn)
            def _():
                term_copy(0, dest, part).wait_send()

    each_send(lambda copy: copy.wait_send())
    each_relay(lambda copy: copy.wait_send())


def body(
    tokens, norm_gain, q_weight, q_bias, k_weight, k_bias, v_weight, v_bias, o_weight, doc_ids
):
    rows, model = tokens.shape
    seq_count = lax.axis_size("seq")
    tp_count = lax.axis_size("tp")
    width = q_weight.shape[1]
    cols = o_weight.shape[1] // tp_count
    reach = min(seq_count - 1, (seq_count * rows // 2 + 2 * rows - 2) // rows)
    chunk = rows // 4
    parts = rows // chunk
    near, far = rope_tables(rows, seq_count)
    hbm = pl.BlockSpec(memory_space=pl.ANY)
    vmem = pl.BlockSpec(memory_space=VMEM)
    slots = reach + 1
    spans = -(-width // (2 * HD))
    kdoc = doc_ids.reshape(seq_count, 1, rows)
    return pl.pallas_call(
        functools.partial(attend, seq_count, tp_count, reach, chunk),
        out_shape=jax.ShapeDtypeStruct((rows, cols), jnp.bfloat16),
        in_specs=[hbm, vmem, hbm, vmem, hbm, vmem, hbm, vmem, hbm, vmem, hbm, vmem],
        out_specs=vmem,
        scratch_shapes=[
            VMEM((rows, model), jnp.bfloat16),
            VMEM((rows, model), jnp.bfloat16),
            VMEM((model, width), jnp.bfloat16),
            VMEM((model, 2 * HD), jnp.bfloat16),
            VMEM(o_weight.shape, jnp.bfloat16),
            VMEM((2, rows, HD), jnp.float32),
            VMEM((rows, width), jnp.bfloat16),
            VMEM((2, rows, HD), jnp.bfloat16),
            VMEM((slots, 2, rows, HD), jnp.bfloat16),
            VMEM((tp_count, rows, cols), jnp.bfloat16),
            VMEM((2, tp_count, rows, cols), jnp.bfloat16),
            VMEM((rows, cols), jnp.float32),
            pltpu.SemaphoreType.DMA((5 + spans,)),
            pltpu.SemaphoreType.DMA((slots,)),
            pltpu.SemaphoreType.DMA((slots,)),
            pltpu.SemaphoreType.DMA((slots,)),
            pltpu.SemaphoreType.DMA((tp_count, parts)),
            pltpu.SemaphoreType.DMA((2, tp_count, parts)),
        ],
        compiler_params=pltpu.CompilerParams(
            collective_id=0, has_side_effects=True, vmem_limit_bytes=56 * 1024 * 1024
        ),
    )(
        tokens, norm_gain, q_weight, q_bias, k_weight, k_bias, v_weight, v_bias, o_weight,
        kdoc, jnp.asarray(near), jnp.asarray(far),
    )


def solution(mesh):
    placed = (
        P("seq", None),
        P(),
        P(None, "tp"),
        P("tp"),
        P(None, "tp"),
        P("tp"),
        P(None, "tp"),
        P("tp"),
        P("tp", None),
        P(),
    )
    return jax.shard_map(
        body, mesh=mesh, in_specs=placed, out_specs=P("seq", "tp"), check_vma=False
    )
```

time: 128 us -> 120 us (0.938); the launches traced: 128 us -> 118 us
  local copies, waits for them, and re-layouts: 6.4 us -> 2.18 us
  Pallas kernels: 119 us -> 116 us
  other arithmetic: 2 us -> 0 us
    pallas_call x1 -> x0, Pallas kernels: 15.4 us -> none  [body(): pl.pallas_call(project, out_shape=(jax.ShapeDtypeStruct((rows, width), jn...]
    pallas_call x1, Pallas kernels: 104 us -> 116 us  [body(): pl.pallas_call(functools.partial(attend, seq_count, tp_count, reach, chun...]
    broadcast_in_dim x3 -> x0, local copies, waits for them, and re-layouts: 3.46 us -> none  [the longest x1 1.33 us: body(): norm_gain[None]]
where the time goes in v2:
time: 120 us; the launch traced here: 118 us
  Pallas kernels  116 us (97%)
  local copies, waits for them, and re-layouts  2.18 us (2%)
    pallas_call x1, Pallas kernels, body(): pl.pallas_call(functools.partial(attend, seq_count, tp_count, reach, chun...  116 us

profile of v2, /device:TPU:5, one launch (start us, length us, event | category | flops | bytes accessed | tf_op | source)
XLA Modules:
  0.0 118.1 jit_solution(10746896596065558767)
XLA Ops:
  0.0 115.9 %shard_map.118 = bf16[512,896]{1,0:T(8,128)(2,1)} custom-call(bf16[512,3584]{1,0:T(8,128)(2,1)} %tokens_hbm.1, f32[3584]{0:T(1024)} %gain_ref.1, bf16[3584,896]{1,0:T(8,128)(2,1)} %wq_hbm.1, f32[896]{0:T(1024)} %qb_ref.1, bf16[3584,128]{1,0:T(8,128)(2,1)} %wk_hbm.1, f32[128]{0:T(128)} %kb_ref.1, bf16[3584,128]{1,0:T(8,128)(2,1)} %wv_hbm.1, f32[128]{0:T(128)} %vb_ref.1, ...), custom_call_target="tpu_custom_call" | custom-call | tf_op jit(solution)/shard_map/pallas_call | solution.py:334
  116.0 2.2 %copy.14 = bf16[512,896]{1,0:T(8,128)(2,1)} copy(bf16[512,896]{1,0:T(8,128)(2,1)} %shard_map.118) | data formatting | bytes 1835008

commit v3 on v2

--- a/solution.py
+++ b/solution.py
@@ -190,14 +190,15 @@
     factor = math.log2(math.e) / HD**0.5
     order = sorted(range(tp_count), key=lambda d: (-abs(2 * d - tp_count + 1), -d))
 
-    def forward(part):
+    def forward(part, first):
         cut = pl.ds(pl.multiple_of(part * chunk, chunk), chunk)
-        for dest in order:
-            for side in (0, 1):
+        for side in (0, 1):
+            chosen = (2 * turn < tp_count) if (side == 0) == first else (2 * turn >= tp_count)
+            for dest in order:
                 inner = (turn > 0) & (dest > turn) if side == 0 else (
                     (turn < tp_count - 1) & (dest < turn))
 
-                @pl.when(inner)
+                @pl.when(inner & chosen)
                 def _():
                     term_copy(side, dest, part).wait_recv()
                     sent[dest, cut] = (
@@ -289,15 +290,19 @@
             def _():
                 term_copy(1, dest, part).start()
 
-    @pl.loop(0, parts + LAG)
+    @pl.loop(0, parts + LAG + 1)
     def _(part):
         @pl.when(part < parts)
         def _():
             piece(part)
 
-        @pl.when(part >= LAG)
-        def _():
-            forward(part - LAG)
+        @pl.when((part >= LAG) & (part < parts + LAG))
+        def _():
+            forward(part - LAG, True)
+
+        @pl.when(part >= LAG + 1)
+        def _():
+            forward(part - LAG - 1, False)
 
     @pl.loop(0, parts)
     def _(part):

time: 120 us -> 101 us (0.84)
  the two profiles are of different devices: /device:TPU:5 before, /device:TPU:28 now
where the time goes in v3:
time: 101 us
  Pallas kernels  99.1 us (98%)
  local copies, waits for them, and re-layouts  2.18 us (2%)
    pallas_call x1, Pallas kernels, body(): pl.pallas_call(functools.partial(attend, seq_count, tp_count, reach, chun...  99.1 us
    unnamed x1, local copies, waits for them, and re-layouts  2.18 us

profile of v3, /device:TPU:28, one launch (start us, length us, event | category | flops | bytes accessed | tf_op | source)
XLA Modules:
  0.0 101.3 jit_solution(16055225733313562510)
XLA Ops:
  0.0 99.1 %shard_map.118 = bf16[512,896]{1,0:T(8,128)(2,1)} custom-call(bf16[512,3584]{1,0:T(8,128)(2,1)} %tokens_hbm.1, f32[3584]{0:T(1024)} %gain_ref.1, bf16[3584,896]{1,0:T(8,128)(2,1)} %wq_hbm.1, f32[896]{0:T(1024)} %qb_ref.1, bf16[3584,128]{1,0:T(8,128)(2,1)} %wk_hbm.1, f32[128]{0:T(128)} %kb_ref.1, bf16[3584,128]{1,0:T(8,128)(2,1)} %wv_hbm.1, f32[128]{0:T(128)} %vb_ref.1, ...), custom_call_target="tpu_custom_call" | custom-call | tf_op jit(solution)/shard_map/pallas_call | solution.py:339
  99.1 2.2 %copy.14 = bf16[512,896]{1,0:T(8,128)(2,1)} copy(bf16[512,896]{1,0:T(8,128)(2,1)} %shard_map.118) | data formatting | bytes 1835008
